TPU v7x, 256 devices: a 8x8x2 block of a 8x8x16 slice. The times are simulated.
256 devices in a mesh: groups: 2 (over z), blk: 64 (over y, x), rep: 2 (over core).
Axes of the slice: x: 8, y: 8, z: 2, core: 2. Of those that a mesh axis runs over, the one named last changes fastest.
The devices are a block of a 8x8x16 slice.
Arguments:
- tokens: bfloat16 [16384, 7168], P(('groups', 'blk', 'rep')), parts along dimension 0, may hold values from -6 to 6
- router_scores: float32 [16384, 8], P(('groups', 'blk', 'rep')), parts along dimension 0, may hold values from -6 to 6
- expert_ids: int32 [16384, 8], P(('groups', 'blk', 'rep')), parts along dimension 0, may hold values from 0 to 255, as said below
- gate_weight: bfloat16 [7168, 32768], P(None, ('blk', 'rep')), may hold values from -0.0625 to 0.0625
- up_weight: bfloat16 [7168, 32768], P(None, ('blk', 'rep')), may hold values from -0.0625 to 0.0625
- down_weight: bfloat16 [32768, 7168], P(('blk', 'rep')), may hold values from -0.125 to 0.125
Outputs:
- moe_out: bfloat16 [16384, 7168], P(('groups', 'blk', 'rep')), parts along dimension 0
There are 2 independent parts, one for each index of `groups`. A program takes and returns all parts, laid end to end along the dimension named above; an argument that names none is the same for every part. Nothing has to cross between parts.
Inputs may be any that keep to these rules, and one draw needn't show every extreme that they name: `expert_ids`: each row names 8 different experts. In the rows of one device (aligned blocks of 64 rows) each expert below 16 is named by at most 2 rows, and in every draw one such expert is named by exactly 2 rows in every block.
All inputs are finite; a program needn't handle non-finite values.
Results may differ from a plain program's by a relative error of at most 0.0068.
Values may be sent and summed in bfloat16 or wider, within the bound.
A program may use at most 128 MiB of HBM per device.

v0:
```python
import functools
import math

import jax
import jax.numpy as jnp
from jax import lax
from jax.experimental import pallas as pl
from jax.experimental.pallas import tpu as pltpu
from jax.sharding import PartitionSpec as P

FF = 2048
CAP = 2
CHUNKS = 4

BATCHES = ((0, 0), (0, 1), (1, 1), (1, 0))
KINDS = "OFLGDBVRC"
ORDER = (
    0, 10, 201, 101, 111, 211, 202, 102, 20, 212, 112, 103, 203, 204, 113, 104, 121, 30,
    105, 213, 221, 122, 205, 114, 300, 231, 400, 131, 214, 222, 232, 605, 115, 123, 215, 505,
    132, 223, 310, 604, 233, 124, 410, 133, 224, 234, 504, 603, 503, 125, 615, 134, 614, 515,
    225, 235, 320, 514, 602, 502, 513, 420, 613, 135, 330, 625, 525, 601, 524, 430, 624, 512,
    612, 535, 635, 501, 623, 534, 634, 523, 611, 511, 633, 533, 522, 622, 700, 710, 532, 632,
    521, 621, 531, 631, 810, 800, 720, 730, 820, 830,
)

route_scale = 2.5

MESH = pl.DeviceIdType.MESH
BF16 = jnp.bfloat16
F32 = jnp.float32


def moe_kernel(
    side,
    gs,
    scores_hbm,
    ids_hbm,
    tok_hbm,
    wg_hbm,
    wu_hbm,
    wd_hbm,
    out_ref,
    scores_ref,
    ids_ref,
    tok,
    wg,
    wu,
    wd,
    mixes,
    send_y,
    recv_y,
    rows,
    oth,
    hidden,
    own_part,
    give,
    take,
    stage,
    from_right,
    from_left,
    oth_sum,
    send_r,
    recv_r,
    out_acc,
    load_sem,
    ys,
    yr,
    xs,
    xr,
    os_,
    ps,
    pr,
    qs,
    qr,
    rs,
    rf,
    rroot,
    tor,
    zs,
    zr,
):
    batches, unit, depth = oth.shape
    count, top = tok.shape[0], ids_ref.shape[0]
    width = depth // CHUNKS
    per_row = side // gs
    half = side // 2
    reach = gs // 2
    slots = gs + 2 * reach
    last = gs - 1
    most = last + reach
    blk = lax.axis_index("blk")
    rep = lax.axis_index("rep")
    y = lax.div(blk, side)
    x = lax.rem(blk, side)
    w = lax.rem(x, gs)
    me = w + reach
    my_half, my_m = lax.div(y, half), lax.rem(y, half)

    def at(yy, xx):
        return {"blk": yy * side + lax.rem(xx + side, side), "rep": rep}

    right = at(y, x + 1)
    left = at(y, x - 1)
    partner = {"rep": 1 - rep}

    def row_of(rel, m):
        return lax.rem(my_half + rel, 2) * half + m

    def remote(src, dst, send, recv, dev):
        return pltpu.make_async_remote_copy(
            src_ref=src, dst_ref=dst, send_sem=send, recv_sem=recv, device_id=dev, device_id_type=MESH
        )

    def arrived(ref, recv):
        remote(ref, ref, recv, recv, partner).wait_recv()

    def sent(ref, send):
        remote(ref, ref, send, send, partner).wait_send()

    def per_cols(body):
        def step(c, _):
            body(pl.ds(pl.multiple_of(c * width, 128), width))
            return 0

        lax.fori_loop(0, CHUNKS, step, 0)

    load_tok = pltpu.make_async_copy(tok_hbm, tok, load_sem.at[0])
    loads = [
        pltpu.make_async_copy(src, dst, load_sem.at[k + 1])
        for k, (src, dst) in enumerate(((wg_hbm, wg), (wu_hbm, wu), (wd_hbm, wd)))
    ]
    tables = [
        pltpu.make_async_copy(src, dst, load_sem.at[4 + k])
        for k, (src, dst) in enumerate(((scores_hbm, scores_ref), (ids_hbm, ids_ref)))
    ]
    for load in tables:
        load.start()
    load_tok.start()

    barrier = pltpu.get_barrier_semaphore()
    for d in range(1, side):
        pl.semaphore_signal(barrier, inc=1, device_id=at(lax.rem(y + d, side), x), device_id_type=MESH)
    for hop in range(1, reach + 1):
        for dev in (at(y, x + hop), at(y, x - hop)):
            pl.semaphore_signal(barrier, inc=1, device_id=dev, device_id_type=MESH)
    pl.semaphore_signal(barrier, inc=1, device_id=partner, device_id_type=MESH)

    for load in tables:
        load.wait()
    spots = side * per_row
    sigmoid = 1.0 / (1.0 + jnp.exp(-scores_ref[...]))
    gates = route_scale * sigmoid / jnp.sum(sigmoid, axis=0, keepdims=True)
    spot = lax.broadcasted_iota(jnp.int32, (spots, count), 0)
    of_half = lax.rem(lax.div(spot, half * per_row) + my_half, 2)
    of_row = of_half * half + lax.rem(lax.div(spot, per_row), half)
    of_expert = of_row * per_row + lax.rem(lax.rem(spot, per_row) + lax.div(x, gs), per_row)
    ids = ids_ref[...]
    weight = jnp.zeros((spots, count), F32)
    hit = jnp.zeros((spots, count), F32)
    for k in range(top):
        same = ids[k : k + 1] == of_expert
        weight += jnp.where(same, gates[k : k + 1], 0.0)
        hit += jnp.where(same, 1.0, 0.0)
    before = lax.broadcasted_iota(jnp.int32, (count, count), 0) < lax.broadcasted_iota(
        jnp.int32, (count, count), 1
    )
    rank = jnp.dot(hit.astype(BF16), jnp.where(before, 1.0, 0.0).astype(BF16), preferred_element_type=F32)
    placed = [jnp.where(rank == s, hit, 0.0) for s in range(CAP)]

    n = half * per_row
    eye = (
        lax.broadcasted_iota(jnp.int32, (n, n), 0) == lax.broadcasted_iota(jnp.int32, (n, n), 1)
    ).astype(F32).astype(BF16)
    for b, (s, rel) in enumerate(BATCHES):
        mix = (placed[s] * weight)[rel * n : (rel + 1) * n]
        mix_hi = mix.astype(BF16)
        mix_lo = (mix - mix_hi.astype(F32)).astype(BF16)
        turned = [
            lax.dot_general(m, eye, (((0,), (0,)), ((), ())), preferred_element_type=F32)
            for m in (mix_hi, mix_lo)
        ]
        mixes[b] = jnp.concatenate(turned, axis=1).astype(BF16)

    load_tok.wait()
    for load in loads:
        load.start()

    for s in range(CAP):
        choose = placed[s].astype(BF16)

        def pack(cols):
            packed = jnp.dot(choose, tok[:, cols], preferred_element_type=F32)
            for p in range(side):
                send_y[s * side + p, :, cols] = packed[p * per_row : (p + 1) * per_row].astype(BF16)

        per_cols(pack)

    pl.semaphore_wait(barrier, side + 2 * reach)

    def exchange(b, source, first, into, send, recv):
        s, rel = BATCHES[b]
        order = (2, 1, 3, 0) if half == 4 else range(half)
        for m in order:
            to = row_of(rel, m)
            src, dst = source.at[first + m], into.at[b * half + my_m]

            def away():
                remote(src, dst, send.at[0], recv.at[b], at(to, x)).start()

            if rel == 0:
                pl.when(my_m != m)(away)

                @pl.when(my_m == m)
                def _():
                    pltpu.make_async_copy(src, dst, recv.at[b]).start()

            else:
                away()

    def forward(b, k, to_right, to_left):
        at_k = b * slots + k
        ref = rows.at[0, at_k]
        if to_right:

            @pl.when(w < last)
            def _():
                remote(ref, ref, xs.at[0], xr.at[at_k], right).start()

        if to_left:

            @pl.when(w > 0)
            def _():
                remote(ref, ref, xs.at[1], xr.at[at_k], left).start()

        remote(ref, rows.at[1, at_k], ps.at[0], pr.at[b], partner).start()

    def y_task(b, _):
        s, rel = BATCHES[b]
        exchange(b, send_y, s * side + rel * half, recv_y, ys, yr)

    def own_task(b, _):
        arrived(recv_y.at[pl.ds(b * half, half)], yr.at[b])

        def body(cols):
            parts = [recv_y[b * half + m, :, cols].astype(F32) for m in range(half)]
            oth[b, :, cols] = jnp.concatenate([p[1:2] for p in parts], axis=0).astype(BF16)
            rows[0, b * slots + me, :, cols] = jnp.concatenate([p[:1] for p in parts], axis=0).astype(BF16)

        per_cols(body)
        near = w < reach
        hop = jnp.where(near, -(w + 1), gs - w)
        slot = b * slots + jnp.where(near, reach + gs + w, w - gs + reach)
        remote(oth.at[b], rows.at[0, slot], os_.at[0], xr.at[slot], at(y, x + hop)).start()
        forward(b, me, True, True)

    def forward_right_task(b, i):
        @pl.when(me - i >= 0)
        def _():
            arrived(rows.at[0, b * slots + me - i], xr.at[b * slots + me - i])
            forward(b, me - i, True, False)

    def forward_left_task(b, i):
        @pl.when(me + i < slots)
        def _():
            arrived(rows.at[0, b * slots + me + i], xr.at[b * slots + me + i])
            forward(b, me + i, False, True)

    many = slots * unit

    loaded = []

    def gate_task(b, _):
        if not loaded:
            loaded.append(b)
            for load in loads:
                load.wait()
        arrived(rows.at[1, pl.ds(b * slots, slots)], pr.at[b])
        block = rows[:, b * slots : (b + 1) * slots].reshape(2 * many, depth)
        gate = jnp.dot(block, wg[...], preferred_element_type=F32)
        up = jnp.dot(block, wu[...], preferred_element_type=F32)
        hidden[...] = (gate / (1.0 + jnp.exp(-gate)) * up).astype(BF16)

    def down_task(b, _):
        def body(cols):
            part = jnp.dot(hidden[...], wd[:, cols], preferred_element_type=F32)
            give[b, :, :, cols] = part[many:].astype(BF16).reshape(slots, unit, width)
            own_part[b, :, :, cols] = part[:many].reshape(slots, unit, width)

        per_cols(body)
        remote(give.at[b], take.at[b], qs.at[0], qr.at[b], partner).start()

    took = []

    def back_task(to_left, b, i):
        if b not in took:
            took.append(b)
            arrived(take.at[b], qr.at[b])

        if True:
            k = me - i if to_left else me + i
            at_k = b * slots + k
            leaf = w == last if to_left else w == 0
            at_end = w == 0 if to_left else w == last
            near = left if to_left else right
            buf = from_right if to_left else from_left
            recv = rroot.at[b] if i == 1 and not to_left else rf.at[at_k]

            @pl.when(k >= 0 if to_left else k < slots)
            def _():
                @pl.when(leaf)
                def _():
                    def body(cols):
                        total = own_part[b, k, :, cols] + take[b, k, :, cols].astype(F32)
                        stage[at_k, :, cols] = total.astype(BF16)

                    per_cols(body)

                @pl.when(jnp.logical_not(leaf))
                def _():
                    arrived(buf.at[at_k], rf.at[at_k])

                    def body(cols):
                        total = own_part[b, k, :, cols] + take[b, k, :, cols].astype(F32)
                        total += buf[at_k, :, cols].astype(F32)
                        stage[at_k, :, cols] = total.astype(BF16)

                    per_cols(body)

                src = stage.at[at_k]

                @pl.when(jnp.logical_not(at_end))
                def _():
                    remote(src, buf.at[at_k], rs.at[0], recv, near).start()

                @pl.when(at_end)
                def _():
                    far = at(y, x - i if to_left else x + i)
                    remote(src, oth_sum.at[b], rs.at[0], tor.at[b], far).start()

    def root_task(b, _):
        at_me = b * slots + me

        def body(cols):
            own_part[b, me, :, cols] += take[b, me, :, cols].astype(F32)

        per_cols(body)

        @pl.when(w < last)
        def _():
            arrived(from_right.at[at_me], rf.at[at_me])

            def body(cols):
                own_part[b, me, :, cols] += from_right[at_me, :, cols].astype(F32)

            per_cols(body)

        @pl.when(w > 0)
        def _():
            arrived(from_left.at[at_me], rroot.at[b])

            def body(cols):
                own_part[b, me, :, cols] += from_left[at_me, :, cols].astype(F32)

            per_cols(body)

        arrived(oth_sum.at[b], tor.at[b])

        def split(cols):
            total = own_part[b, me, :, cols]
            other = oth_sum[b, :, cols].astype(F32)
            for m in range(half):
                pair = jnp.concatenate([total[m : m + 1], other[m : m + 1]], axis=0)
                send_r[b * half + m, :, cols] = pair.astype(BF16)

        per_cols(split)
        exchange(b, send_r, b * half, recv_r, zs, zr)

    combined = []

    def combine_task(b, _):
        arrived(recv_r.at[pl.ds(b * half, half)], zr.at[b])
        mix = mixes[b]
        begin, end = not combined, len(combined) == batches - 1
        combined.append(b)

        def body(cols):
            parts = [recv_r[b * half + m, :, cols].astype(F32) for m in range(half)]
            block = jnp.concatenate(parts + parts, axis=0).astype(BF16)
            total = jnp.dot(mix, block, preferred_element_type=F32)
            if not begin:
                total += out_acc[:, cols]
            if end:
                out_ref[:, cols] = total.astype(BF16)
            else:
                out_acc[:, cols] = total

        per_cols(body)

    tasks = (
        own_task,
        forward_right_task,
        forward_left_task,
        gate_task,
        down_task,
        functools.partial(back_task, True),
        functools.partial(back_task, False),
        root_task,
        combine_task,
    )
    for b in range(batches):
        y_task(b, 0)
    for code in ORDER:
        kind, b, i = code // 100, code // 10 % 10, code % 10
        with jax.named_scope(f"{KINDS[kind]}{b}{i}"):
            tasks[kind](b, i)

    with jax.named_scope("drain"):
        away = CAP * (side - 1)
        sent(send_y.at[pl.ds(0, away)], ys.at[0])
        sent(send_r.at[pl.ds(0, away)], zs.at[0])
        sent(oth, os_.at[0])
        sent(rows.at[0], ps.at[0])
        sent(give, qs.at[0])
        sent(stage.at[pl.ds(0, batches * (slots - 1))], rs.at[0])
        for pos in range(gs):

            @pl.when(w == pos)
            def _():
                if pos < last:
                    sent(rows.at[0, pl.ds(0, batches * (pos + reach + 1))], xs.at[0])
                if pos > 0:
                    sent(rows.at[0, pl.ds(0, batches * (slots - reach - pos))], xs.at[1])


def shards(tokens, router_scores, expert_ids, gate_weight, up_weight, down_weight):
    blk_count = lax.axis_size("blk")
    rep_count = lax.axis_size("rep")
    count, depth = tokens.shape
    units = gate_weight.shape[1]
    window = blk_count * rep_count * units // FF
    gs = blk_count // window
    side = math.isqrt(blk_count)
    per_row = side // gs

    batches = len(BATCHES)
    slots = 2 * gs
    unit = side // 2
    many = slots * unit
    vmem = pl.BlockSpec(memory_space=pltpu.VMEM)
    hbm = pl.BlockSpec(memory_space=pltpu.HBM)
    dma = pltpu.SemaphoreType.DMA
    pieces = pltpu.VMEM((CAP * side, per_row, depth), BF16)
    blocks = pltpu.VMEM((batches * slots, unit, depth), BF16)
    parts = (batches, slots, unit, depth)
    single = pltpu.VMEM((batches, unit, depth), BF16)
    large = [
        pltpu.with_memory_space_constraint(a, pltpu.HBM)
        for a in (router_scores.T, expert_ids.T, tokens, gate_weight, up_weight, down_weight)
    ]
    return pl.pallas_call(
        functools.partial(moe_kernel, side, gs),
        out_shape=jax.ShapeDtypeStruct((count, depth), BF16),
        in_specs=[hbm] * len(large),
        out_specs=vmem,
        scratch_shapes=[
            pltpu.VMEM(router_scores.shape[::-1], F32),
            pltpu.VMEM(expert_ids.shape[::-1], jnp.int32),
            pltpu.VMEM((count, depth), BF16),
            pltpu.VMEM(gate_weight.shape, BF16),
            pltpu.VMEM(up_weight.shape, BF16),
            pltpu.VMEM(down_weight.shape, BF16),
            pltpu.VMEM((batches, count, side * per_row), BF16),
            pieces,
            pieces,
            pltpu.VMEM((2, batches * slots, unit, depth), BF16),
            single,
            pltpu.VMEM((2 * many, units), BF16),
            pltpu.VMEM(parts, F32),
            pltpu.VMEM(parts, BF16),
            pltpu.VMEM(parts, BF16),
            blocks,
            blocks,
            blocks,
            single,
            pieces,
            pieces,
            pltpu.VMEM((count, depth), F32),
            dma((6,)),
            dma((1,)),
            dma((batches,)),
            dma((2,)),
            dma((batches * slots,)),
            dma((1,)),
            dma((1,)),
            dma((batches,)),
            dma((1,)),
            dma((batches,)),
            dma((1,)),
            dma((batches * slots,)),
            dma((batches,)),
            dma((batches,)),
            dma((1,)),
            dma((batches,)),
        ],
        compiler_params=pltpu.CompilerParams(
            collective_id=0, has_side_effects=True, vmem_limit_bytes=44 * 1024 * 1024
        ),
    )(*large)


def solution(mesh):
    placed = (
        P(("groups", "blk", "rep"), None),
        P(("groups", "blk", "rep"), None),
        P(("groups", "blk", "rep"), None),
        P(None, ("blk", "rep")),
        P(None, ("blk", "rep")),
        P(("blk", "rep"), None),
    )
    return jax.shard_map(
        shards,
        mesh=mesh,
        in_specs=placed,
        out_specs=P(("groups", "blk", "rep"), None),
        check_vma=False,
    )
```

profile of v0, /device:TPU:514, one launch (start us, length us, event | category | flops | bytes accessed | tf_op | source)
XLA Modules:
  0.0 95.9 jit_solution(5197826419269354233)
XLA Ops:
  0.0 95.0 %shard_map.64 = bf16[64,7168]{1,0:T(8,128)(2,1)S(1)} custom-call(f32[8,64]{1,0:T(8,128)} %bitcast.2, s32[8,64]{1,0:T(8,128)} %bitcast.3, bf16[64,7168]{1,0:T(8,128)(2,1)} %tok_hbm.1, bf16[7168,256]{1,0:T(8,128)(2,1)} %wg_hbm.1, bf16[7168,256]{1,0:T(8,128)(2,1)} %wu_hbm.1, bf16[256,7168]{1,0:T(8,128)(2,1)} %wd_hbm.1), custom_call_target="tpu_custom_call" | custom-call | tf_op jit(solution)/shard_map/pallas_call | solution.py:460
  95.0 0.9 copy.8
where the time goes:
time: 96 us; the launch traced here: 95.9 us
  Pallas kernels  95 us (99%)
    pallas_call x1, Pallas kernels, shards(): pl.pallas_call(functools.partial(moe_kernel, side, gs), out_shape=jax.Sha...  95 us

commit v1 on v0

--- a/solution.py
+++ b/solution.py
@@ -15,12 +15,11 @@
 BATCHES = ((0, 0), (0, 1), (1, 1), (1, 0))
 KINDS = "OFLGDBVRC"
 ORDER = (
-    0, 10, 201, 101, 111, 211, 202, 102, 20, 212, 112, 103, 203, 204, 113, 104, 121, 30,
-    105, 213, 221, 122, 205, 114, 300, 231, 400, 131, 214, 222, 232, 605, 115, 123, 215, 505,
-    132, 223, 310, 604, 233, 124, 410, 133, 224, 234, 504, 603, 503, 125, 615, 134, 614, 515,
-    225, 235, 320, 514, 602, 502, 513, 420, 613, 135, 330, 625, 525, 601, 524, 430, 624, 512,
-    612, 535, 635, 501, 623, 534, 634, 523, 611, 511, 633, 533, 522, 622, 700, 710, 532, 632,
-    521, 621, 531, 631, 810, 800, 720, 730, 820, 830,
+    0, 10, 101, 20, 102, 201, 111, 211, 103, 121, 202, 112, 203, 122, 204, 212, 205, 30,
+    113, 300, 123, 400, 213, 214, 131, 221, 605, 215, 222, 231, 310, 132, 223, 410, 232, 604,
+    615, 224, 233, 133, 503, 603, 614, 225, 234, 602, 320, 613, 502, 420, 612, 235, 601, 330,
+    501, 625, 430, 513, 624, 635, 623, 512, 700, 634, 523, 622, 511, 633, 611, 533, 522, 800,
+    632, 532, 621, 521, 710, 631, 531, 720, 730, 810, 820, 830,
 )
 
 route_scale = 2.5
@@ -56,8 +55,7 @@
     give,
     take,
     stage,
-    from_right,
-    from_left,
+    came,
     oth_sum,
     send_r,
     recv_r,
@@ -94,17 +92,21 @@
     x = lax.rem(blk, side)
     w = lax.rem(x, gs)
     me = w + reach
-    my_half, my_m = lax.div(y, half), lax.rem(y, half)
+    my_half, my_m = lax.rem(y, 2), lax.div(y, 2)
 
     def at(yy, xx):
         return {"blk": yy * side + lax.rem(xx + side, side), "rep": rep}
 
-    right = at(y, x + 1)
-    left = at(y, x - 1)
+    sign = jnp.where(w < reach, 1, -1)
+    inner = jnp.logical_and(w > 0, w < last)
+    up_side = jnp.where(w < reach, 0, 1)
+    depth_in = jnp.minimum(w, last - w)
+    up = at(y, x + sign)
+    down = at(y, x - sign)
     partner = {"rep": 1 - rep}
 
     def row_of(rel, m):
-        return lax.rem(my_half + rel, 2) * half + m
+        return m * 2 + lax.rem(my_half + rel, 2)
 
     def remote(src, dst, send, recv, dev):
         return pltpu.make_async_remote_copy(
@@ -152,7 +154,7 @@
     gates = route_scale * sigmoid / jnp.sum(sigmoid, axis=0, keepdims=True)
     spot = lax.broadcasted_iota(jnp.int32, (spots, count), 0)
     of_half = lax.rem(lax.div(spot, half * per_row) + my_half, 2)
-    of_row = of_half * half + lax.rem(lax.div(spot, per_row), half)
+    of_row = lax.rem(lax.div(spot, per_row), half) * 2 + of_half
     of_expert = of_row * per_row + lax.rem(lax.rem(spot, per_row) + lax.div(x, gs), per_row)
     ids = ids_ref[...]
     weight = jnp.zeros((spots, count), F32)
@@ -217,20 +219,17 @@
             else:
                 away()
 
-    def forward(b, k, to_right, to_left):
+    def forward(b, k, to_up, to_down):
         at_k = b * slots + k
         ref = rows.at[0, at_k]
-        if to_right:
-
-            @pl.when(w < last)
+        if to_up:
+            remote(ref, ref, xs.at[0], xr.at[at_k], up).start()
+
+        if to_down:
+
+            @pl.when(inner)
             def _():
-                remote(ref, ref, xs.at[0], xr.at[at_k], right).start()
-
-        if to_left:
-
-            @pl.when(w > 0)
-            def _():
-                remote(ref, ref, xs.at[1], xr.at[at_k], left).start()
+                remote(ref, ref, xs.at[1], xr.at[at_k], down).start()
 
         remote(ref, rows.at[1, at_k], ps.at[0], pr.at[b], partner).start()
 
@@ -253,17 +252,30 @@
         remote(oth.at[b], rows.at[0, slot], os_.at[0], xr.at[slot], at(y, x + hop)).start()
         forward(b, me, True, True)
 
-    def forward_right_task(b, i):
-        @pl.when(me - i >= 0)
-        def _():
-            arrived(rows.at[0, b * slots + me - i], xr.at[b * slots + me - i])
-            forward(b, me - i, True, False)
-
-    def forward_left_task(b, i):
-        @pl.when(me + i < slots)
-        def _():
-            arrived(rows.at[0, b * slots + me + i], xr.at[b * slots + me + i])
-            forward(b, me + i, False, True)
+    def when_far(i, most_in, body):
+        if i > most_in:
+            pl.when(inner)(body)
+        else:
+            body()
+
+    def forward_up_task(b, i):
+        def body():
+            k = me - sign * i
+            arrived(rows.at[0, b * slots + k], xr.at[b * slots + k])
+            forward(b, k, True, False)
+
+        when_far(i, reach, body)
+
+    def forward_down_task(b, i):
+        def body():
+            k = me + sign * i
+            arrived(rows.at[0, b * slots + k], xr.at[b * slots + k])
+            forward(b, k, False, True)
+
+        if i == most:
+            pl.when(jnp.logical_not(inner))(body)
+        else:
+            body()
 
     many = slots * unit
 
@@ -285,57 +297,74 @@
             part = jnp.dot(hidden[...], wd[:, cols], preferred_element_type=F32)
             give[b, :, :, cols] = part[many:].astype(BF16).reshape(slots, unit, width)
             own_part[b, :, :, cols] = part[:many].reshape(slots, unit, width)
+            ours, theirs = give.at[b, :, :, cols], take.at[b, :, :, cols]
+            remote(ours, theirs, qs.at[0], qr.at[b], partner).start()
 
         per_cols(body)
-        remote(give.at[b], take.at[b], qs.at[0], qr.at[b], partner).start()
 
     took = []
 
-    def back_task(to_left, b, i):
+    def partial_sum(b, k, side_in, at_in):
+        at_k = b * slots + k
+
+        def body(cols):
+            total = own_part[b, k, :, cols] + take[b, k, :, cols].astype(F32)
+            if at_in:
+                total += came.at[side_in][at_k, :, cols].astype(F32)
+            stage[at_k, :, cols] = total.astype(BF16)
+
+        if at_in:
+            arrived(came.at[side_in, at_k], rf.at[at_k])
+        per_cols(body)
+
+    def taken(b):
         if b not in took:
             took.append(b)
             arrived(take.at[b], qr.at[b])
 
-        if True:
-            k = me - i if to_left else me + i
+    def back_down_task(b, i):
+        taken(b)
+
+        def body():
+            k = me - sign * i
             at_k = b * slots + k
-            leaf = w == last if to_left else w == 0
-            at_end = w == 0 if to_left else w == last
-            near = left if to_left else right
-            buf = from_right if to_left else from_left
-            recv = rroot.at[b] if i == 1 and not to_left else rf.at[at_k]
-
-            @pl.when(k >= 0 if to_left else k < slots)
+            partial_sum(b, k, up_side, True)
+            src = stage.at[at_k]
+            recv = rroot.at[up_side, b] if i == 1 else rf.at[at_k]
+
+            @pl.when(inner)
             def _():
-                @pl.when(leaf)
-                def _():
-                    def body(cols):
-                        total = own_part[b, k, :, cols] + take[b, k, :, cols].astype(F32)
-                        stage[at_k, :, cols] = total.astype(BF16)
-
-                    per_cols(body)
-
-                @pl.when(jnp.logical_not(leaf))
-                def _():
-                    arrived(buf.at[at_k], rf.at[at_k])
-
-                    def body(cols):
-                        total = own_part[b, k, :, cols] + take[b, k, :, cols].astype(F32)
-                        total += buf[at_k, :, cols].astype(F32)
-                        stage[at_k, :, cols] = total.astype(BF16)
-
-                    per_cols(body)
-
-                src = stage.at[at_k]
-
-                @pl.when(jnp.logical_not(at_end))
-                def _():
-                    remote(src, buf.at[at_k], rs.at[0], recv, near).start()
-
-                @pl.when(at_end)
-                def _():
-                    far = at(y, x - i if to_left else x + i)
-                    remote(src, oth_sum.at[b], rs.at[0], tor.at[b], far).start()
+                remote(src, came.at[up_side, at_k], rs.at[0], recv, down).start()
+
+            @pl.when(jnp.logical_not(inner))
+            def _():
+                remote(src, oth_sum.at[b], rs.at[0], tor.at[b], at(y, x - sign * i)).start()
+
+        when_far(i, reach, body)
+
+    def back_up_task(b, i):
+        taken(b)
+        k = me + sign * i
+        at_k = b * slots + k
+        recv = rroot.at[1 - up_side, b] if i == 1 else rf.at[at_k]
+
+        @pl.when(jnp.logical_not(inner))
+        def _():
+            partial_sum(b, k, 1 - up_side, False)
+
+        if i < most:
+
+            @pl.when(inner)
+            def _():
+                partial_sum(b, k, 1 - up_side, True)
+
+        def body():
+            remote(stage.at[at_k], came.at[1 - up_side, at_k], rs.at[0], recv, up).start()
+
+        if i == most:
+            pl.when(jnp.logical_not(inner))(body)
+        else:
+            body()
 
     def root_task(b, _):
         at_me = b * slots + me
@@ -345,24 +374,16 @@
 
         per_cols(body)
 
-        @pl.when(w < last)
-        def _():
-            arrived(from_right.at[at_me], rf.at[at_me])
+        def add(side_in):
+            arrived(came.at[side_in, at_me], rroot.at[side_in, b])
 
             def body(cols):
-                own_part[b, me, :, cols] += from_right[at_me, :, cols].astype(F32)
+                own_part[b, me, :, cols] += came.at[side_in][at_me, :, cols].astype(F32)
 
             per_cols(body)
 
-        @pl.when(w > 0)
-        def _():
-            arrived(from_left.at[at_me], rroot.at[b])
-
-            def body(cols):
-                own_part[b, me, :, cols] += from_left[at_me, :, cols].astype(F32)
-
-            per_cols(body)
-
+        add(up_side)
+        pl.when(inner)(lambda: add(1 - up_side))
         arrived(oth_sum.at[b], tor.at[b])
 
         def split(cols):
@@ -398,12 +419,12 @@
 
     tasks = (
         own_task,
-        forward_right_task,
-        forward_left_task,
+        forward_up_task,
+        forward_down_task,
         gate_task,
         down_task,
-        functools.partial(back_task, True),
-        functools.partial(back_task, False),
+        back_down_task,
+        back_up_task,
         root_task,
         combine_task,
     )
@@ -422,12 +443,11 @@
         sent(rows.at[0], ps.at[0])
         sent(give, qs.at[0])
         sent(stage.at[pl.ds(0, batches * (slots - 1))], rs.at[0])
-        for pos in range(gs):
-
-            @pl.when(w == pos)
+        for pos in range(reach):
+
+            @pl.when(depth_in == pos)
             def _():
-                if pos < last:
-                    sent(rows.at[0, pl.ds(0, batches * (pos + reach + 1))], xs.at[0])
+                sent(rows.at[0, pl.ds(0, batches * (pos + reach + 1))], xs.at[0])
                 if pos > 0:
                     sent(rows.at[0, pl.ds(0, batches * (slots - reach - pos))], xs.at[1])
 
@@ -479,8 +499,7 @@
             pltpu.VMEM(parts, BF16),
             pltpu.VMEM(parts, BF16),
             blocks,
-            blocks,
-            blocks,
+            pltpu.VMEM((2, batches * slots, unit, depth), BF16),
             single,
             pieces,
             pieces,
@@ -497,7 +516,7 @@
             dma((batches,)),
             dma((1,)),
             dma((batches * slots,)),
-            dma((batches,)),
+            dma((2, batches)),
             dma((batches,)),
             dma((1,)),
             dma((batches,)),

time: 96 us -> 92.7 us (0.966)
  Pallas kernels: 95 us -> 91.6 us
    pallas_call x1, Pallas kernels: 95 us -> 91.6 us  [shards(): pl.pallas_call(functools.partial(moe_kernel, side, gs), out_shape=jax.Sha...]
where the time goes in v1:
time: 92.7 us; the launch traced here: 92.5 us
  Pallas kernels  91.6 us (99%)
  local copies, waits for them, and re-layouts  0.93 us (1%)
    pallas_call x1, Pallas kernels, shards(): pl.pallas_call(functools.partial(moe_kernel, side, gs), out_shape=jax.Sha...  91.6 us

profile of v1, /device:TPU:514, one launch (start us, length us, event | category | flops | bytes accessed | tf_op | source)
XLA Modules:
  0.0 92.5 jit_solution(14862222892744099109)
XLA Ops:
  0.0 91.6 %shard_map.64 = bf16[64,7168]{1,0:T(8,128)(2,1)S(1)} custom-call(f32[8,64]{1,0:T(8,128)} %bitcast.2, s32[8,64]{1,0:T(8,128)} %bitcast.3, bf16[64,7168]{1,0:T(8,128)(2,1)} %tok_hbm.1, bf16[7168,256]{1,0:T(8,128)(2,1)} %wg_hbm.1, bf16[7168,256]{1,0:T(8,128)(2,1)} %wu_hbm.1, bf16[256,7168]{1,0:T(8,128)(2,1)} %wd_hbm.1), custom_call_target="tpu_custom_call" | custom-call | tf_op jit(solution)/shard_map/pallas_call | solution.py:480
  91.6 0.9 copy.8

commit v2 on v1

v2 whole, which is shorter than its diff:
```python
import functools
import math

import jax
import jax.numpy as jnp
from jax import lax
from jax.experimental import pallas as pl
from jax.experimental.pallas import tpu as pltpu
from jax.sharding import PartitionSpec as P

FF = 2048
CAP = 2
CHUNKS = 4

BATCHES = ((0, 0), (0, 1), (1, 1), (1, 0))
KINDS = "OFLGDBVRCUE"
ORDER = (
    0, 10, 201, 101, 20, 202, 102, 211, 30, 103, 111, 112, 203, 113, 121, 204, 212, 131,
    122, 205, 213, 300, 900, 400, 214, 1000, 221, 215, 132, 605, 231, 222, 310, 910, 410, 1010,
    123, 223, 232, 604, 615, 133, 224, 233, 603, 503, 614, 225, 234, 613, 602, 320, 502, 513,
    920, 235, 612, 420, 601, 1020, 330, 930, 625, 430, 1030, 624, 501, 623, 512, 523, 635, 634,
    622, 511, 633, 522, 533, 700, 611, 521, 632, 532, 621, 710, 531, 631, 720, 730, 800, 810,
    820, 830,
)

route_scale = 2.5

MESH = pl.DeviceIdType.MESH
BF16 = jnp.bfloat16
F32 = jnp.float32


def moe_kernel(
    side,
    gs,
    scores_hbm,
    ids_hbm,
    tok_hbm,
    wg_hbm,
    wu_hbm,
    wd_hbm,
    out_ref,
    scores_ref,
    ids_ref,
    tok,
    wg,
    wu,
    wd,
    mixes,
    send_y,
    recv_y,
    rows,
    oth,
    gate_acc,
    hidden,
    own_part,
    give,
    take,
    stage,
    came,
    oth_sum,
    send_r,
    recv_r,
    out_acc,
    load_sem,
    ys,
    yr,
    xs,
    xr,
    os_,
    ps,
    pr,
    qs,
    qr,
    rs,
    rf,
    rroot,
    tor,
    zs,
    zr,
):
    batches, unit, depth = oth.shape
    count, top = tok.shape[0], ids_ref.shape[0]
    width = depth // CHUNKS
    per_row = side // gs
    half = side // 2
    reach = gs // 2
    slots = gs + 2 * reach
    last = gs - 1
    most = last + reach
    blk = lax.axis_index("blk")
    rep = lax.axis_index("rep")
    y = lax.div(blk, side)
    x = lax.rem(blk, side)
    w = lax.rem(x, gs)
    me = w + reach
    my_half, my_m = lax.rem(y, 2), lax.div(y, 2)

    def at(yy, xx):
        return {"blk": yy * side + lax.rem(xx + side, side), "rep": rep}

    sign = jnp.where(w < reach, 1, -1)
    inner = jnp.logical_and(w > 0, w < last)
    up_side = jnp.where(w < reach, 0, 1)
    depth_in = jnp.minimum(w, last - w)
    up = at(y, x + sign)
    down = at(y, x - sign)
    partner = {"rep": 1 - rep}

    def row_of(rel, m):
        return m * 2 + lax.rem(my_half + rel, 2)

    def remote(src, dst, send, recv, dev):
        return pltpu.make_async_remote_copy(
            src_ref=src, dst_ref=dst, send_sem=send, recv_sem=recv, device_id=dev, device_id_type=MESH
        )

    def arrived(ref, recv):
        remote(ref, ref, recv, recv, partner).wait_recv()

    def sent(ref, send):
        remote(ref, ref, send, send, partner).wait_send()

    def per_cols(body):
        def step(c, _):
            body(pl.ds(pl.multiple_of(c * width, 128), width))
            return 0

        lax.fori_loop(0, CHUNKS, step, 0)

    load_tok = pltpu.make_async_copy(tok_hbm, tok, load_sem.at[0])
    loads = [
        pltpu.make_async_copy(src, dst, load_sem.at[k + 1])
        for k, (src, dst) in enumerate(((wg_hbm, wg), (wu_hbm, wu), (wd_hbm, wd)))
    ]
    tables = [
        pltpu.make_async_copy(src, dst, load_sem.at[4 + k])
        for k, (src, dst) in enumerate(((scores_hbm, scores_ref), (ids_hbm, ids_ref)))
    ]
    for load in tables:
        load.start()
    load_tok.start()

    barrier = pltpu.get_barrier_semaphore()
    for d in range(1, side):
        pl.semaphore_signal(barrier, inc=1, device_id=at(lax.rem(y + d, side), x), device_id_type=MESH)
    for hop in range(1, reach + 1):
        for dev in (at(y, x + hop), at(y, x - hop)):
            pl.semaphore_signal(barrier, inc=1, device_id=dev, device_id_type=MESH)
    pl.semaphore_signal(barrier, inc=1, device_id=partner, device_id_type=MESH)

    for load in tables:
        load.wait()
    spots = side * per_row
    sigmoid = 1.0 / (1.0 + jnp.exp(-scores_ref[...]))
    gates = route_scale * sigmoid / jnp.sum(sigmoid, axis=0, keepdims=True)
    spot = lax.broadcasted_iota(jnp.int32, (spots, count), 0)
    of_half = lax.rem(lax.div(spot, half * per_row) + my_half, 2)
    of_row = lax.rem(lax.div(spot, per_row), half) * 2 + of_half
    of_expert = of_row * per_row + lax.rem(lax.rem(spot, per_row) + lax.div(x, gs), per_row)
    ids = ids_ref[...]
    weight = jnp.zeros((spots, count), F32)
    hit = jnp.zeros((spots, count), F32)
    for k in range(top):
        same = ids[k : k + 1] == of_expert
        weight += jnp.where(same, gates[k : k + 1], 0.0)
        hit += jnp.where(same, 1.0, 0.0)
    before = lax.broadcasted_iota(jnp.int32, (count, count), 0) < lax.broadcasted_iota(
        jnp.int32, (count, count), 1
    )
    rank = jnp.dot(hit.astype(BF16), jnp.where(before, 1.0, 0.0).astype(BF16), preferred_element_type=F32)
    placed = [jnp.where(rank == s, hit, 0.0) for s in range(CAP)]

    load_tok.wait()
    for load in loads:
        load.start()

    def pack_rank(s):
        choose = placed[s].astype(BF16)

        def pack(cols):
            packed = jnp.dot(choose, tok[:, cols], preferred_element_type=F32)
            for p in range(side):
                send_y[s * side + p, :, cols] = packed[p * per_row : (p + 1) * per_row].astype(BF16)

        per_cols(pack)

    pack_rank(0)
    pl.semaphore_wait(barrier, side + 2 * reach)

    def exchange(b, source, first, into, send, recv):
        rel = BATCHES[b][1]
        dst = into.at[b * half + my_m]
        near = lambda d: -min(2 * d + rel, side - 2 * d - rel)
        for d in sorted(range(1 - rel, half), key=near):
            m = lax.rem(my_m + d + rel * my_half, half)
            remote(source.at[first + m], dst, send.at[0], recv.at[b], at(row_of(rel, m), x)).start()
        if rel == 0:
            pltpu.make_async_copy(source.at[first + my_m], dst, recv.at[b]).start()

    def forward(b, k, to_up, to_down):
        at_k = b * slots + k
        ref = rows.at[0, at_k]
        if to_up:
            remote(ref, ref, xs.at[0], xr.at[at_k], up).start()

        if to_down:

            @pl.when(inner)
            def _():
                remote(ref, ref, xs.at[1], xr.at[at_k], down).start()

        remote(ref, rows.at[1, at_k], ps.at[0], pr.at[b], partner).start()

    def y_task(b, _):
        s, rel = BATCHES[b]
        exchange(b, send_y, s * side + rel * half, recv_y, ys, yr)

    def own_task(b, _):
        arrived(recv_y.at[pl.ds(b * half, half)], yr.at[b])

        def body(cols):
            parts = [recv_y[b * half + m, :, cols].astype(F32) for m in range(half)]
            oth[b, :, cols] = jnp.concatenate([p[1:2] for p in parts], axis=0).astype(BF16)
            rows[0, b * slots + me, :, cols] = jnp.concatenate([p[:1] for p in parts], axis=0).astype(BF16)

        per_cols(body)
        near = w < reach
        hop = jnp.where(near, -(w + 1), gs - w)
        slot = b * slots + jnp.where(near, reach + gs + w, w - gs + reach)
        remote(oth.at[b], rows.at[0, slot], os_.at[0], xr.at[slot], at(y, x + hop)).start()
        forward(b, me, True, True)

    def when_far(i, most_in, body):
        if i > most_in:
            pl.when(inner)(body)
        else:
            body()

    def forward_up_task(b, i):
        def body():
            k = me - sign * i
            arrived(rows.at[0, b * slots + k], xr.at[b * slots + k])
            forward(b, k, True, False)

        when_far(i, reach, body)

    def forward_down_task(b, i):
        def body():
            k = me + sign * i
            arrived(rows.at[0, b * slots + k], xr.at[b * slots + k])
            forward(b, k, False, True)

        if i == most:
            pl.when(jnp.logical_not(inner))(body)
        else:
            body()

    many = slots * unit

    loaded = []

    def gate_task(b, _):
        if not loaded:
            loaded.append(b)
            for load in loads:
                load.wait()
        arrived(rows.at[1, pl.ds(b * slots, slots)], pr.at[b])
        block = rows[:, b * slots : (b + 1) * slots].reshape(2 * many, depth)
        gate_acc[...] = jnp.dot(block, wg[...], preferred_element_type=F32)

    def up_task(b, _):
        block = rows[:, b * slots : (b + 1) * slots].reshape(2 * many, depth)
        gate = gate_acc[...]
        up = jnp.dot(block, wu[...], preferred_element_type=F32)
        hidden[...] = (gate / (1.0 + jnp.exp(-gate)) * up).astype(BF16)

    def down_task(part_at, b, _):
        def step(c, _):
            cols = pl.ds(pl.multiple_of(c * width, 128), width)
            part = jnp.dot(hidden[...], wd[:, cols], preferred_element_type=F32)
            give[b, :, :, cols] = part[many:].astype(BF16).reshape(slots, unit, width)
            own_part[b, :, :, cols] = part[:many].reshape(slots, unit, width)
            ours, theirs = give.at[b, :, :, cols], take.at[b, :, :, cols]
            remote(ours, theirs, qs.at[0], qr.at[b], partner).start()
            return 0

        lax.fori_loop(part_at * CHUNKS // 2, (part_at + 1) * CHUNKS // 2, step, 0)

    took = []

    def partial_sum(b, k, side_in, at_in):
        at_k = b * slots + k

        def body(cols):
            total = own_part[b, k, :, cols] + take[b, k, :, cols].astype(F32)
            if at_in:
                total += came.at[side_in][at_k, :, cols].astype(F32)
            stage[at_k, :, cols] = total.astype(BF16)

        if at_in:
            arrived(came.at[side_in, at_k], rf.at[at_k])
        per_cols(body)

    def taken(b):
        if b not in took:
            took.append(b)
            arrived(take.at[b], qr.at[b])

    def back_down_task(b, i):
        taken(b)

        def body():
            k = me - sign * i
            at_k = b * slots + k
            partial_sum(b, k, up_side, True)
            src = stage.at[at_k]
            recv = rroot.at[up_side, b] if i == 1 else rf.at[at_k]

            @pl.when(inner)
            def _():
                remote(src, came.at[up_side, at_k], rs.at[0], recv, down).start()

            @pl.when(jnp.logical_not(inner))
            def _():
                remote(src, oth_sum.at[b], rs.at[0], tor.at[b], at(y, x - sign * i)).start()

        when_far(i, reach, body)

    def back_up_task(b, i):
        taken(b)
        k = me + sign * i
        at_k = b * slots + k
        recv = rroot.at[1 - up_side, b] if i == 1 else rf.at[at_k]

        @pl.when(jnp.logical_not(inner))
        def _():
            partial_sum(b, k, 1 - up_side, False)

        if i < most:

            @pl.when(inner)
            def _():
                partial_sum(b, k, 1 - up_side, True)

        def body():
            remote(stage.at[at_k], came.at[1 - up_side, at_k], rs.at[0], recv, up).start()

        if i == most:
            pl.when(jnp.logical_not(inner))(body)
        else:
            body()

    def root_task(b, _):
        at_me = b * slots + me

        def body(cols):
            own_part[b, me, :, cols] += take[b, me, :, cols].astype(F32)

        per_cols(body)

        def add(side_in):
            arrived(came.at[side_in, at_me], rroot.at[side_in, b])

            def body(cols):
                own_part[b, me, :, cols] += came.at[side_in][at_me, :, cols].astype(F32)

            per_cols(body)

        add(up_side)
        pl.when(inner)(lambda: add(1 - up_side))
        arrived(oth_sum.at[b], tor.at[b])

        def split(cols):
            total = own_part[b, me, :, cols]
            other = oth_sum[b, :, cols].astype(F32)
            for m in range(half):
                pair = jnp.concatenate([total[m : m + 1], other[m : m + 1]], axis=0)
                send_r[b * half + m, :, cols] = pair.astype(BF16)

        per_cols(split)
        exchange(b, send_r, b * half, recv_r, zs, zr)

    combined = []

    def combine_task(b, _):
        arrived(recv_r.at[pl.ds(b * half, half)], zr.at[b])
        mix = mixes[b]
        begin, end = not combined, len(combined) == batches - 1
        combined.append(b)

        def body(cols):
            parts = [recv_r[b * half + m, :, cols].astype(F32) for m in range(half)]
            block = jnp.concatenate(parts + parts, axis=0).astype(BF16)
            total = jnp.dot(mix, block, preferred_element_type=F32)
            if not begin:
                total += out_acc[:, cols]
            if end:
                out_ref[:, cols] = total.astype(BF16)
            else:
                out_acc[:, cols] = total

        per_cols(body)

    tasks = (
        own_task,
        forward_up_task,
        forward_down_task,
        gate_task,
        functools.partial(down_task, 0),
        back_down_task,
        back_up_task,
        root_task,
        combine_task,
        up_task,
        functools.partial(down_task, 1),
    )
    for s in range(CAP):
        if s > 0:
            pack_rank(s)
        for b in range(batches):
            if BATCHES[b][0] == s:
                y_task(b, 0)

    n = half * per_row
    eye = (
        lax.broadcasted_iota(jnp.int32, (n, n), 0) == lax.broadcasted_iota(jnp.int32, (n, n), 1)
    ).astype(F32).astype(BF16)
    for b, (s, rel) in enumerate(BATCHES):
        mix = (placed[s] * weight)[rel * n : (rel + 1) * n]
        mix_hi = mix.astype(BF16)
        mix_lo = (mix - mix_hi.astype(F32)).astype(BF16)
        turned = [
            lax.dot_general(m, eye, (((0,), (0,)), ((), ())), preferred_element_type=F32)
            for m in (mix_hi, mix_lo)
        ]
        mixes[b] = jnp.concatenate(turned, axis=1).astype(BF16)

    for code in ORDER:
        kind, b, i = code // 100, code // 10 % 10, code % 10
        with jax.named_scope(f"{KINDS[kind]}{b}{i}"):
            tasks[kind](b, i)

    with jax.named_scope("drain"):
        away = CAP * (side - 1)
        sent(send_y.at[pl.ds(0, away)], ys.at[0])
        sent(send_r.at[pl.ds(0, away)], zs.at[0])
        sent(oth, os_.at[0])
        sent(rows.at[0], ps.at[0])
        sent(give, qs.at[0])
        sent(stage.at[pl.ds(0, batches * (slots - 1))], rs.at[0])
        for pos in range(reach):

            @pl.when(depth_in == pos)
            def _():
                sent(rows.at[0, pl.ds(0, batches * (pos + reach + 1))], xs.at[0])
                if pos > 0:
                    sent(rows.at[0, pl.ds(0, batches * (slots - reach - pos))], xs.at[1])


def shards(tokens, router_scores, expert_ids, gate_weight, up_weight, down_weight):
    blk_count = lax.axis_size("blk")
    rep_count = lax.axis_size("rep")
    count, depth = tokens.shape
    units = gate_weight.shape[1]
    window = blk_count * rep_count * units // FF
    gs = blk_count // window
    side = math.isqrt(blk_count)
    per_row = side // gs

    batches = len(BATCHES)
    slots = 2 * gs
    unit = side // 2
    many = slots * unit
    vmem = pl.BlockSpec(memory_space=pltpu.VMEM)
    hbm = pl.BlockSpec(memory_space=pltpu.HBM)
    dma = pltpu.SemaphoreType.DMA
    pieces = pltpu.VMEM((CAP * side, per_row, depth), BF16)
    blocks = pltpu.VMEM((batches * slots, unit, depth), BF16)
    parts = (batches, slots, unit, depth)
    single = pltpu.VMEM((batches, unit, depth), BF16)
    large = [
        pltpu.with_memory_space_constraint(a, pltpu.HBM)
        for a in (router_scores.T, expert_ids.T, tokens, gate_weight, up_weight, down_weight)
    ]
    return pl.pallas_call(
        functools.partial(moe_kernel, side, gs),
        out_shape=jax.ShapeDtypeStruct((count, depth), BF16),
        in_specs=[hbm] * len(large),
        out_specs=vmem,
        scratch_shapes=[
            pltpu.VMEM(router_scores.shape[::-1], F32),
            pltpu.VMEM(expert_ids.shape[::-1], jnp.int32),
            pltpu.VMEM((count, depth), BF16),
            pltpu.VMEM(gate_weight.shape, BF16),
            pltpu.VMEM(up_weight.shape, BF16),
            pltpu.VMEM(down_weight.shape, BF16),
            pltpu.VMEM((batches, count, side * per_row), BF16),
            pieces,
            pieces,
            pltpu.VMEM((2, batches * slots, unit, depth), BF16),
            single,
            pltpu.VMEM((2 * many, units), F32),
            pltpu.VMEM((2 * many, units), BF16),
            pltpu.VMEM(parts, F32),
            pltpu.VMEM(parts, BF16),
            pltpu.VMEM(parts, BF16),
            blocks,
            pltpu.VMEM((2, batches * slots, unit, depth), BF16),
            single,
            pieces,
            pieces,
            pltpu.VMEM((count, depth), F32),
            dma((6,)),
            dma((1,)),
            dma((batches,)),
            dma((2,)),
            dma((batches * slots,)),
            dma((1,)),
            dma((1,)),
            dma((batches,)),
            dma((1,)),
            dma((batches,)),
            dma((1,)),
            dma((batches * slots,)),
            dma((2, batches)),
            dma((batches,)),
            dma((1,)),
            dma((batches,)),
        ],
        compiler_params=pltpu.CompilerParams(
            collective_id=0, has_side_effects=True, vmem_limit_bytes=44 * 1024 * 1024
        ),
    )(*large)


def solution(mesh):
    placed = (
        P(("groups", "blk", "rep"), None),
        P(("groups", "blk", "rep"), None),
        P(("groups", "blk", "rep"), None),
        P(None, ("blk", "rep")),
        P(None, ("blk", "rep")),
        P(("blk", "rep"), None),
    )
    return jax.shard_map(
        shards,
        mesh=mesh,
        in_specs=placed,
        out_specs=P(("groups", "blk", "rep"), None),
        check_vma=False,
    )
```

time: 92.7 us -> 91 us (0.982)
  Pallas kernels: 91.6 us -> 90 us
    pallas_call x1, Pallas kernels: 91.6 us -> 90 us  [shards(): pl.pallas_call(functools.partial(moe_kernel, side, gs), out_shape=jax.Sha...]
where the time goes in v2:
time: 91 us; the launch traced here: 90.9 us
  Pallas kernels  90 us (99%)
  local copies, waits for them, and re-layouts  0.93 us (1%)
    pallas_call x1, Pallas kernels, shards(): pl.pallas_call(functools.partial(moe_kernel, side, gs), out_shape=jax.Sha...  90 us

profile of v2, /device:TPU:514, one launch (start us, length us, event | category | flops | bytes accessed | tf_op | source)
XLA Modules:
  0.0 90.9 jit_solution(12412652745856477385)
XLA Ops:
  0.0 90.0 %shard_map.64 = bf16[64,7168]{1,0:T(8,128)(2,1)S(1)} custom-call(f32[8,64]{1,0:T(8,128)} %bitcast.2, s32[8,64]{1,0:T(8,128)} %bitcast.3, bf16[64,7168]{1,0:T(8,128)(2,1)} %tok_hbm.1, bf16[7168,256]{1,0:T(8,128)(2,1)} %wg_hbm.1, bf16[7168,256]{1,0:T(8,128)(2,1)} %wu_hbm.1, bf16[256,7168]{1,0:T(8,128)(2,1)} %wd_hbm.1), custom_call_target="tpu_custom_call" | custom-call | tf_op jit(solution)/shard_map/pallas_call | solution.py:486
  90.0 0.9 %copy.8 = bf16[64,7168]{1,0:T(8,128)(2,1)} copy(bf16[64,7168]{1,0:T(8,128)(2,1)S(1)} %shard_map.64) | data formatting | bytes 1835008
